TPU v7x, 256 devices: a whole 4x4x8 slice. The times are simulated.
256 devices in a mesh: wide: 64 (over z_lo, x, y, core), narrow: 4 (over z_hi).
Axes of the slice: x: 4, y: 4, z: 8 (z_hi: 4, z_lo: 2; z = z_hi * 2 + z_lo), core: 2. Of those that a mesh axis runs over, the one named last changes fastest.
Arguments:
- queries: bfloat16 [131072, 768], P(('wide', 'narrow')), may hold values from -150 to 150
- documents: bfloat16 [8192, 768], P(('wide', 'narrow')), may hold values from -5 to 5
- positives: int32 [131072], P(('wide', 'narrow')), may hold values from 0 to 8191
Outputs:
- losses: float32 [131072], P(('wide', 'narrow'))
- query_grad: bfloat16 [131072, 768], P(('wide', 'narrow'))
All inputs are finite; a program needn't handle non-finite values. Where the computation divides by a largest or mean magnitude, that divisor is 1e-20 or more.
Results may differ from a plain program's by a relative error of at most 0.005.
Values may be sent and summed in bfloat16 or wider, within the bound.
A program may use at most 64 MiB of HBM per device.

v0:
```python
import jax
import jax.numpy as jnp
from jax import lax
from jax.sharding import PartitionSpec as P

span = 512


def in_order(parts, dim):
    shape = list(parts.shape[1:])
    shape[dim] *= parts.shape[0]
    return jnp.moveaxis(parts, 0, dim).reshape(shape)


def copy_for_each(shard, axis):
    peers = lax.axis_size(axis)
    return lax.all_to_all(
        jnp.broadcast_to(shard[None], (peers, *shard.shape)), axis, 0, 0, tiled=True
    )


def gathered_copies(shard, axis, dim):
    return in_order(copy_for_each(shard, axis), dim)


def block_scores(queries, codes, scales, temper):
    raw = lax.dot_general(
        queries, codes, (((1,), (1,)), ((), ())), preferred_element_type=jnp.float32
    )
    return raw * scales[None, :] * temper


def hits(positives, start, rows):
    column_ids = lax.broadcasted_iota(jnp.int32, (positives.shape[0], rows), 1) + start
    return column_ids == positives[:, None]


def sweep(update, carry, codes, scales):
    rows = codes.shape[0]

    def step(index, state):
        begin = (index * span).astype(jnp.int32)
        piece = lax.dynamic_slice_in_dim(codes, begin, span, 0)
        piece_scales = lax.dynamic_slice_in_dim(scales, begin, span, 0)
        return update(state, piece, piece_scales, begin)

    return lax.fori_loop(0, rows // span, step, carry)


def shards(queries, documents, positives):
    width = queries.shape[1]
    temper = width ** (-0.5)
    doc_values = documents.astype(jnp.float32)
    scales = jnp.max(jnp.abs(doc_values), axis=1) + 1e-06
    codes = (doc_values / scales[:, None]).astype(jnp.bfloat16)
    count = queries.shape[0]

    def totals(carry, piece, piece_scales, start):
        run_max, run_sum, chosen = carry
        scores = block_scores(queries, piece, piece_scales, temper)
        new_max = jnp.maximum(run_max, jnp.max(scores, axis=1))
        run_sum = run_sum * jnp.exp(run_max - new_max) + jnp.sum(
            jnp.exp(scores - new_max[:, None]), axis=1
        )
        found = hits(positives, start, piece.shape[0])
        chosen = chosen + jnp.sum(jnp.where(found, scores, 0.0), axis=1)
        return (new_max, run_sum, chosen)

    init = (
        jnp.full((count,), -1e30, jnp.float32),
        jnp.zeros((count,), jnp.float32),
        jnp.zeros((count,), jnp.float32),
    )
    grad_init = jnp.zeros((count, width), jnp.float32)

    def make_gradient(lse):

        def gradient(total, piece, piece_scales, start):
            scores = block_scores(queries, piece, piece_scales, temper)
            probs = jnp.exp(scores - lse[:, None])
            found = hits(positives, start, piece.shape[0]).astype(jnp.float32)
            weights = ((probs - found) * piece_scales[None, :]).astype(jnp.bfloat16)
            return total + jnp.dot(weights, piece, preferred_element_type=jnp.float32)

        return gradient

    group_codes, group_scales = (
        gathered_copies(codes, "narrow", 0),
        gathered_copies(scales.astype(jnp.bfloat16), "narrow", 0).astype(scales.dtype),
    )
    pieces = (
        lax.all_gather(group_codes, "wide", axis=0, tiled=True),
        lax.all_gather(group_scales.astype(jnp.bfloat16), "wide", axis=0, tiled=True).astype(
            jnp.float32
        ),
    )
    run_max, run_sum, chosen = sweep(totals, init, pieces[0], pieces[1])
    lse = run_max + jnp.log(run_sum)
    gradient = make_gradient(lse)
    pieces = (
        lax.all_gather(group_codes, "wide", axis=0, tiled=True),
        lax.all_gather(group_scales.astype(jnp.bfloat16), "wide", axis=0, tiled=True).astype(
            jnp.float32
        ),
    )
    total = sweep(gradient, grad_init, pieces[0], pieces[1])
    losses = lse - chosen
    return (losses, (total * temper).astype(jnp.bfloat16))


def solution(mesh):
    placed = (P(("wide", "narrow"), None), P(("wide", "narrow"), None), P(("wide", "narrow")))
    return jax.shard_map(
        shards,
        mesh=mesh,
        in_specs=placed,
        out_specs=(P(("wide", "narrow")), P(("wide", "narrow"), None)),
        check_vma=False,
    )
```

profile of v0, /device:TPU:1, one launch (start us, length us, event | category | flops | bytes accessed | tf_op | source)
XLA Modules:
  0.0 248.1 jit_solution(2231653285240883626)
XLA Ops:
  9.0 17.0 %all_to_all.11 = bf16[4,32,768]{2,1,0:T(8,128)(2,1)} all-to-all(bf16[4,32,768]{2,1,0:T(8,128)(2,1)S(1)} %broadcast_in_dim.47), channel_id=1, replica_groups=mesh['wide'=64,'narrow'=4] {'narrow'}, dimensions={0} | all-to-all | bytes 393216 | tf_op jit(solution)/shard_map/all_to_all | solution.py:17
  26.6 3.3 %all-to-all-start.1 = ((bf16[4,1,32]{2,1,0:T(2,128)(2,1)}), bf16[4,1,32]{2,1,0:T(2,128)(2,1)S(1)}, u32[]{:S(2)}, u32[]{:S(2)}) async-start(bf16[4,1,32]{2,1,0:T(2,128)(2,1)} %broadcast_in_dim.48), calls=%async_computation.1 | async-start | bytes 4096 | tf_op jit(solution)/shard_map/all_to_all | solution.py:17
  30.0 6.5 %all-to-all-done.1 = bf16[4,1,32]{2,1,0:T(2,128)(2,1)S(1)} async-done(((bf16[4,1,32]{2,1,0:T(2,128)(2,1)}), bf16[4,1,32]{2,1,0:T(2,128)(2,1)S(1)}, u32[]{:S(2)}, u32[]{:S(2)}) %all-to-all-start.1) | async-done | bytes 288 | tf_op jit(solution)/shard_map/all_to_all | solution.py:17
  36.5 85.3 %all-gather = bf16[64,1,128]{2,1,0:T(2,128)(2,1)S(1)} all-gather(bf16[1,1,128]{2,1,0:T(2,128)(2,1)S(1)} %reshape.33), channel_id=1, replica_groups=mesh['wide'=64,'narrow'=4] {'wide'}, dimensions={0}, use_global_device_ids=true | all-gather | bytes 16640 | tf_op jit(solution)/shard_map/all_gather | solution.py:93
  121.9 22.5 %all-gather.3.cloned.1.call-done = bf16[8192,768]{1,0:T(8,128)(2,1)} async-done(((bf16[128,768]{1,0:T(8,128)(2,1)}), bf16[8192,768]{1,0:T(8,128)(2,1)}) %all-gather.3.cloned.1.call-update) | async-done | bytes 12582928 | tf_op jit(solution)/shard_map/all_gather | solution.py:92
  144.4 38.9 %while.32 = (s32[]{:T(128)}, f32[512]{0:T(512)S(1)}, f32[512]{0:T(512)S(1)}, f32[512]{0:T(512)S(1)}, bf16[8192,768]{1,0:T(8,128)(2,1)}, /*index=5*/bf16[512,768]...) while((s32[]{:T(128)}, f32[512]{0:T(512)S(1)}, ...), condition=%wide.region_5.6_spmd.clone, body=%wide.region_1.5_spmd.clone.sunk | while | flops 404753920 | bytes 3725534 | solution.py:47
  144.4 2.0 fusion.41
  146.9 2.0 fusion.41
  149.3 2.0 fusion.41
  154.2 2.0 fusion.41
  159.0 2.0 fusion.41
  163.9 2.0 fusion.41
  168.8 2.0 fusion.41
  173.6 2.0 fusion.41
  178.5 2.0 fusion.41
  183.9 56.4 %while.33 = (s32[]{:T(128)}, f32[512,768]{1,0:T(8,128)S(1)}, bf16[8192,768]{1,0:T(8,128)(2,1)}, bf16[512,768]{1,0:T(8,128)(2,1)}, f32[8192]{0:T(1024)S(1)}, /*in...) while((s32[]{:T(128)}, f32[512,768]{1,0:T(8,128)S(1)}, ...), condition=%wide.region_7.8_spmd.clone, body=%wide.region_6.7_spmd.clone.sunk | while | flops 808190464 | bytes 5523124 | solution.py:47
  183.9 3.4 %select_add_fusion.5 = f32[512,768]{1,0:T(8,128)S(1)} fusion(f32[512,768]{1,0:T(8,128)S(1)} %get-tuple-element.514, bf16[512,768]{1,0:T(8,128)(2,1)} %get-tuple-element.527, bf16[8192,768]{1,0:T(8,128)(2,1)} %get-tuple-element.526, s32[]{:T(128)S(6)} %select_n.35, pred[]{:T(512)S(6)} %compare.7, f32[512]{0:T(512)S(1)} %dynamic_slice.48, ...), kind=kOutput, calls=%fused_computation.14.clone.1 | convolution fusion | flops 808189952 | bytes 5516800 | tf_op jit(solution)/shard_map/while/body/eval_jaxpr/dot_general | solution.py:83
  187.5 3.4 %select_add_fusion.5 = f32[512,768]{1,0:T(8,128)S(1)} fusion(f32[512,768]{1,0:T(8,128)S(1)} %get-tuple-element.514, bf16[512,768]{1,0:T(8,128)(2,1)} %get-tuple-element.527, bf16[8192,768]{1,0:T(8,128)(2,1)} %get-tuple-element.526, s32[]{:T(128)S(6)} %select_n.35, pred[]{:T(512)S(6)} %compare.7, f32[512]{0:T(512)S(1)} %dynamic_slice.48, ...), kind=kOutput, calls=%fused_computation.14.clone.1 | convolution fusion | flops 808189952 | bytes 5516800 | tf_op jit(solution)/shard_map/while/body/eval_jaxpr/dot_general | solution.py:83
  191.0 3.4 %select_add_fusion.5 = f32[512,768]{1,0:T(8,128)S(1)} fusion(f32[512,768]{1,0:T(8,128)S(1)} %get-tuple-element.514, bf16[512,768]{1,0:T(8,128)(2,1)} %get-tuple-element.527, bf16[8192,768]{1,0:T(8,128)(2,1)} %get-tuple-element.526, s32[]{:T(128)S(6)} %select_n.35, pred[]{:T(512)S(6)} %compare.7, f32[512]{0:T(512)S(1)} %dynamic_slice.48, ...), kind=kOutput, calls=%fused_computation.14.clone.1 | convolution fusion | flops 808189952 | bytes 5516800 | tf_op jit(solution)/shard_map/while/body/eval_jaxpr/dot_general | solution.py:83
  194.5 3.4 %select_add_fusion.5 = f32[512,768]{1,0:T(8,128)S(1)} fusion(f32[512,768]{1,0:T(8,128)S(1)} %get-tuple-element.514, bf16[512,768]{1,0:T(8,128)(2,1)} %get-tuple-element.527, bf16[8192,768]{1,0:T(8,128)(2,1)} %get-tuple-element.526, s32[]{:T(128)S(6)} %select_n.35, pred[]{:T(512)S(6)} %compare.7, f32[512]{0:T(512)S(1)} %dynamic_slice.48, ...), kind=kOutput, calls=%fused_computation.14.clone.1 | convolution fusion | flops 808189952 | bytes 5516800 | tf_op jit(solution)/shard_map/while/body/eval_jaxpr/dot_general | solution.py:83
  198.0 3.4 %select_add_fusion.5 = f32[512,768]{1,0:T(8,128)S(1)} fusion(f32[512,768]{1,0:T(8,128)S(1)} %get-tuple-element.514, bf16[512,768]{1,0:T(8,128)(2,1)} %get-tuple-element.527, bf16[8192,768]{1,0:T(8,128)(2,1)} %get-tuple-element.526, s32[]{:T(128)S(6)} %select_n.35, pred[]{:T(512)S(6)} %compare.7, f32[512]{0:T(512)S(1)} %dynamic_slice.48, ...), kind=kOutput, calls=%fused_computation.14.clone.1 | convolution fusion | flops 808189952 | bytes 5516800 | tf_op jit(solution)/shard_map/while/body/eval_jaxpr/dot_general | solution.py:83
  201.6 3.4 %select_add_fusion.5 = f32[512,768]{1,0:T(8,128)S(1)} fusion(f32[512,768]{1,0:T(8,128)S(1)} %get-tuple-element.514, bf16[512,768]{1,0:T(8,128)(2,1)} %get-tuple-element.527, bf16[8192,768]{1,0:T(8,128)(2,1)} %get-tuple-element.526, s32[]{:T(128)S(6)} %select_n.35, pred[]{:T(512)S(6)} %compare.7, f32[512]{0:T(512)S(1)} %dynamic_slice.48, ...), kind=kOutput, calls=%fused_computation.14.clone.1 | convolution fusion | flops 808189952 | bytes 5516800 | tf_op jit(solution)/shard_map/while/body/eval_jaxpr/dot_general | solution.py:83
  205.1 3.4 %select_add_fusion.5 = f32[512,768]{1,0:T(8,128)S(1)} fusion(f32[512,768]{1,0:T(8,128)S(1)} %get-tuple-element.514, bf16[512,768]{1,0:T(8,128)(2,1)} %get-tuple-element.527, bf16[8192,768]{1,0:T(8,128)(2,1)} %get-tuple-element.526, s32[]{:T(128)S(6)} %select_n.35, pred[]{:T(512)S(6)} %compare.7, f32[512]{0:T(512)S(1)} %dynamic_slice.48, ...), kind=kOutput, calls=%fused_computation.14.clone.1 | convolution fusion | flops 808189952 | bytes 5516800 | tf_op jit(solution)/shard_map/while/body/eval_jaxpr/dot_general | solution.py:83
  208.6 3.5 %select_add_fusion.5 = f32[512,768]{1,0:T(8,128)S(1)} fusion(f32[512,768]{1,0:T(8,128)S(1)} %get-tuple-element.514, bf16[512,768]{1,0:T(8,128)(2,1)} %get-tuple-element.527, bf16[8192,768]{1,0:T(8,128)(2,1)} %get-tuple-element.526, s32[]{:T(128)S(6)} %select_n.35, pred[]{:T(512)S(6)} %compare.7, f32[512]{0:T(512)S(1)} %dynamic_slice.48, ...), kind=kOutput, calls=%fused_computation.14.clone.1 | convolution fusion | flops 808189952 | bytes 5516800 | tf_op jit(solution)/shard_map/while/body/eval_jaxpr/dot_general | solution.py:83
  212.2 3.4 %select_add_fusion.5 = f32[512,768]{1,0:T(8,128)S(1)} fusion(f32[512,768]{1,0:T(8,128)S(1)} %get-tuple-element.514, bf16[512,768]{1,0:T(8,128)(2,1)} %get-tuple-element.527, bf16[8192,768]{1,0:T(8,128)(2,1)} %get-tuple-element.526, s32[]{:T(128)S(6)} %select_n.35, pred[]{:T(512)S(6)} %compare.7, f32[512]{0:T(512)S(1)} %dynamic_slice.48, ...), kind=kOutput, calls=%fused_computation.14.clone.1 | convolution fusion | flops 808189952 | bytes 5516800 | tf_op jit(solution)/shard_map/while/body/eval_jaxpr/dot_general | solution.py:83
  215.7 3.4 %select_add_fusion.5 = f32[512,768]{1,0:T(8,128)S(1)} fusion(f32[512,768]{1,0:T(8,128)S(1)} %get-tuple-element.514, bf16[512,768]{1,0:T(8,128)(2,1)} %get-tuple-element.527, bf16[8192,768]{1,0:T(8,128)(2,1)} %get-tuple-element.526, s32[]{:T(128)S(6)} %select_n.35, pred[]{:T(512)S(6)} %compare.7, f32[512]{0:T(512)S(1)} %dynamic_slice.48, ...), kind=kOutput, calls=%fused_computation.14.clone.1 | convolution fusion | flops 808189952 | bytes 5516800 | tf_op jit(solution)/shard_map/while/body/eval_jaxpr/dot_general | solution.py:83
  219.3 3.4 %select_add_fusion.5 = f32[512,768]{1,0:T(8,128)S(1)} fusion(f32[512,768]{1,0:T(8,128)S(1)} %get-tuple-element.514, bf16[512,768]{1,0:T(8,128)(2,1)} %get-tuple-element.527, bf16[8192,768]{1,0:T(8,128)(2,1)} %get-tuple-element.526, s32[]{:T(128)S(6)} %select_n.35, pred[]{:T(512)S(6)} %compare.7, f32[512]{0:T(512)S(1)} %dynamic_slice.48, ...), kind=kOutput, calls=%fused_computation.14.clone.1 | convolution fusion | flops 808189952 | bytes 5516800 | tf_op jit(solution)/shard_map/while/body/eval_jaxpr/dot_general | solution.py:83
  222.8 3.4 %select_add_fusion.5 = f32[512,768]{1,0:T(8,128)S(1)} fusion(f32[512,768]{1,0:T(8,128)S(1)} %get-tuple-element.514, bf16[512,768]{1,0:T(8,128)(2,1)} %get-tuple-element.527, bf16[8192,768]{1,0:T(8,128)(2,1)} %get-tuple-element.526, s32[]{:T(128)S(6)} %select_n.35, pred[]{:T(512)S(6)} %compare.7, f32[512]{0:T(512)S(1)} %dynamic_slice.48, ...), kind=kOutput, calls=%fused_computation.14.clone.1 | convolution fusion | flops 808189952 | bytes 5516800 | tf_op jit(solution)/shard_map/while/body/eval_jaxpr/dot_general | solution.py:83
  226.3 3.4 %select_add_fusion.5 = f32[512,768]{1,0:T(8,128)S(1)} fusion(f32[512,768]{1,0:T(8,128)S(1)} %get-tuple-element.514, bf16[512,768]{1,0:T(8,128)(2,1)} %get-tuple-element.527, bf16[8192,768]{1,0:T(8,128)(2,1)} %get-tuple-element.526, s32[]{:T(128)S(6)} %select_n.35, pred[]{:T(512)S(6)} %compare.7, f32[512]{0:T(512)S(1)} %dynamic_slice.48, ...), kind=kOutput, calls=%fused_computation.14.clone.1 | convolution fusion | flops 808189952 | bytes 5516800 | tf_op jit(solution)/shard_map/while/body/eval_jaxpr/dot_general | solution.py:83
  229.8 3.4 %select_add_fusion.5 = f32[512,768]{1,0:T(8,128)S(1)} fusion(f32[512,768]{1,0:T(8,128)S(1)} %get-tuple-element.514, bf16[512,768]{1,0:T(8,128)(2,1)} %get-tuple-element.527, bf16[8192,768]{1,0:T(8,128)(2,1)} %get-tuple-element.526, s32[]{:T(128)S(6)} %select_n.35, pred[]{:T(512)S(6)} %compare.7, f32[512]{0:T(512)S(1)} %dynamic_slice.48, ...), kind=kOutput, calls=%fused_computation.14.clone.1 | convolution fusion | flops 808189952 | bytes 5516800 | tf_op jit(solution)/shard_map/while/body/eval_jaxpr/dot_general | solution.py:83
  233.4 3.4 %select_add_fusion.5 = f32[512,768]{1,0:T(8,128)S(1)} fusion(f32[512,768]{1,0:T(8,128)S(1)} %get-tuple-element.514, bf16[512,768]{1,0:T(8,128)(2,1)} %get-tuple-element.527, bf16[8192,768]{1,0:T(8,128)(2,1)} %get-tuple-element.526, s32[]{:T(128)S(6)} %select_n.35, pred[]{:T(512)S(6)} %compare.7, f32[512]{0:T(512)S(1)} %dynamic_slice.48, ...), kind=kOutput, calls=%fused_computation.14.clone.1 | convolution fusion | flops 808189952 | bytes 5516800 | tf_op jit(solution)/shard_map/while/body/eval_jaxpr/dot_general | solution.py:83
  236.9 3.4 %select_add_fusion.5 = f32[512,768]{1,0:T(8,128)S(1)} fusion(f32[512,768]{1,0:T(8,128)S(1)} %get-tuple-element.514, bf16[512,768]{1,0:T(8,128)(2,1)} %get-tuple-element.527, bf16[8192,768]{1,0:T(8,128)(2,1)} %get-tuple-element.526, s32[]{:T(128)S(6)} %select_n.35, pred[]{:T(512)S(6)} %compare.7, f32[512]{0:T(512)S(1)} %dynamic_slice.48, ...), kind=kOutput, calls=%fused_computation.14.clone.1 | convolution fusion | flops 808189952 | bytes 5516800 | tf_op jit(solution)/shard_map/while/body/eval_jaxpr/dot_general | solution.py:83
  (183 shorter events, 25.5 us)
Async XLA Ops:
  7.2 137.2 %all-gather.3.cloned.1.call-start = ((), (), s32[]{:S(2)}) async-start(), calls=%async_computation.2 | async-start | bytes 12779520 | tf_op jit(solution)/shard_map/all_gather | solution.py:92
  26.6 9.8 %all-to-all-start.1 = ((bf16[4,1,32]{2,1,0:T(2,128)(2,1)}), bf16[4,1,32]{2,1,0:T(2,128)(2,1)S(1)}, u32[]{:S(2)}, u32[]{:S(2)}) async-start(bf16[4,1,32]{2,1,0:T(2,128)(2,1)} %broadcast_in_dim.48), calls=%async_computation.1 | async-start | bytes 4096 | tf_op jit(solution)/shard_map/all_to_all | solution.py:17
  144.4 2.1 copy-start
  146.8 2.1 copy-start
  149.2 2.1 copy-start
  151.6 2.1 copy-start
  154.1 2.1 copy-start
  156.5 2.1 copy-start
  158.9 2.1 copy-start
  161.4 2.1 copy-start
  163.8 2.1 copy-start
  166.2 2.1 copy-start
  168.7 2.1 copy-start
  171.1 2.1 copy-start
  173.5 2.1 copy-start
  176.0 2.1 copy-start
  178.4 2.1 copy-start
  180.8 2.1 copy-start
Sparse Core Ops, SparseCore 0:
  26.1 118.1 all-gather.2
where the time goes:
time: 249 us; the launch traced here: 248 us
  blocking collectives  102 us (41%)
  matrix products  86.3 us (35%)
  waiting for transfers between devices  29 us (12%)
  between operations  14.1 us (6%)
  other arithmetic  8.24 us (3%)
  starting transfers between devices  3.38 us (1%)
  local copies, waits for them, and re-layouts  3.36 us (1%)
    all_gather x1, blocking collectives, shards(): lax.all_gather(group_scales.astype(jnp.bfloat16), 'wide', axis=0, tiled=T...  85.3 us
    dot_general x16, matrix products, gradient(): return total + jnp.dot(weights, piece, preferred_element_type=jnp.float32)  54.5 us
    dot_general x16, matrix products, block_scores(): lax.dot_general(queries, codes, (((1,), (1,)), ((), ())), preferred_eleme...  31.8 us
    all_gather x1, waiting for transfers between devices, shards(): lax.all_gather(group_codes, 'wide', axis=0, tiled=True)  22.5 us
    all_to_all x1, blocking collectives, copy_for_each(): lax.all_to_all(jnp.broadcast_to(shard[None], (peers, *shard.shape)), axis...  17 us
    all_to_all x1, waiting for transfers between devices, copy_for_each(): lax.all_to_all(jnp.broadcast_to(shard[None], (peers, *shard.shape)), axis...  6.46 us
  transfers between devices with their start and end apart: 2, of which 2 were waited for; matrix products, arithmetic and copies ran while one was open for 0% of the time, Pallas kernels for 0%

commit v1 on v0

v1 whole, which is shorter than its diff:
```python
import jax
import jax.numpy as jnp
from jax import lax
from jax.experimental import pallas as pl
from jax.experimental.pallas import tpu as pltpu
from jax.sharding import PartitionSpec as P

LOG2E = 1.4426950408889634
MESH = pl.DeviceIdType.MESH
NX, NY, NZ = 4, 4, 8
RB = 32
SLOTS = 8
Y_COLS = (0, 256)
X_COLS = (256, 256)
XW_COLS = (256, 512)
W_COLS = (512, 256)
ZB_COLS = (0, 512)
W_OFF = (0, 1, 3, 2)
ROWS = 256


def kernel(
    n_copies,
    q_ref,
    d_ref,
    p_ref,
    loss_ref,
    grad_ref,
    buf,
    sbuf,
    pos,
    run_max,
    run_sum,
    chosen,
    acc,
    picked,
    s_a,
    s_b,
    send_sem,
    recv_sem,
):
    wide = lax.axis_index("wide")
    narrow = lax.axis_index("narrow")
    core = lax.rem(wide, 2)
    y = lax.rem(wide // 2, NY)
    x = lax.rem(wide // 8, NX)
    z = narrow * 2 + wide // 32
    width = q_ref.shape[1]
    temper = width**-0.5

    def xm(d):
        return lax.rem(x + d + NX, NX)

    def ym(d):
        return lax.rem(y + d + NY, NY)

    def zm(d):
        return lax.rem(z + d + NZ, NZ)

    def dev(xx, yy, zz, cc):
        return ((lax.rem(zz, 2) * NX + xx) * NY + yy) * 2 + cc, zz // 2

    at_x = lambda d: dev(xm(d), y, z, core)
    at_y = lambda d: dev(x, ym(d), z, core)
    at_z = lambda d: dev(x, y, zm(d), core)
    sibling = dev(x, y, z, 1 - core)

    docs = d_ref[...].astype(jnp.float32)
    scale = jnp.max(jnp.abs(docs), axis=1, keepdims=True) + 1e-06
    mine = (z * 2 + core) * NX + x
    my_rows = pl.ds(pl.multiple_of(y * RB, RB), RB)
    buf[mine, my_rows, :] = (docs / scale).astype(jnp.bfloat16)
    lane = lax.broadcasted_iota(jnp.int32, (RB, 128), 1)
    row = lax.broadcasted_iota(jnp.int32, (RB, 128), 0)
    sbuf[z, core, x * NY + y] = jnp.sum(
        jnp.where(lane == row + y * RB, scale, 0.0), axis=0, keepdims=True
    )

    barrier = pltpu.get_barrier_semaphore()
    peers = (
        [sibling]
        + [at_x(d) for d in (1, 2, 3)]
        + [at_y(d) for d in (1, 2, 3)]
        + [at_z(d) for d in range(1, NZ)]
    )
    for peer in peers:
        pl.semaphore_signal(barrier, inc=1, device_id=peer, device_id_type=MESH)
    pl.semaphore_wait(barrier, len(peers))

    index = {}
    draining = []

    def copy_of(key, ref, peer):
        i = index.setdefault(key, len(index))
        return pltpu.make_async_remote_copy(
            src_ref=ref,
            dst_ref=ref,
            send_sem=send_sem.at[i],
            recv_sem=recv_sem.at[i],
            device_id=peer,
            device_id_type=MESH,
        )

    def send(key, ref, peer):
        copy = copy_of(key, ref, peer)
        if draining:
            copy.wait_send()
        else:
            copy.start()

    def arrive(key, ref):
        if not draining:
            copy_of(key, ref, sibling).wait_recv()

    def cell(plane, xx):
        return (plane * 2 + core) * NX + xx

    def block(plane, xx, yy, cols, first=0, rows=RB):
        start = pl.multiple_of(yy * RB + first, 16)
        return buf.at[cell(plane, xx), pl.ds(start, rows), pl.ds(*cols)]

    def y_group(plane, xx, cols, first=0, rows=NY * RB):
        return buf.at[cell(plane, xx), pl.ds(first, rows), pl.ds(*cols)]

    def x_group(plane, yy, cols, first=0, many=NX):
        start = pl.multiple_of(yy * RB, RB)
        return buf.at[
            pl.ds(cell(plane, 0) + first, many), pl.ds(start, RB), pl.ds(*cols)
        ]

    def dz(s):
        return 0 if s == 0 else (-((s + 1) // 2) if s % 2 else s // 2)

    def plane_at(s):
        return zm(dz(s))

    def x_cols(s):
        return XW_COLS if s == 0 else X_COLS

    def stage_a(s):
        p = plane_at(s)
        for d in (1, -1):
            send(("Xy", s, d), block(p, x, y, x_cols(s)), at_y(d))
            send(("Yx", s, d), block(p, x, y, Y_COLS), at_x(d))

    def stage_b(s):
        p = plane_at(s)
        for d in (1, -1):
            half = 0 if d == 1 else RB // 2
            arrive(("Xy", s, d), block(p, x, ym(-d), x_cols(s)))
            send(
                ("XyF", s, d),
                block(p, x, ym(-d), x_cols(s), half, RB // 2),
                at_y(d),
            )
            arrive(("Yx", s, d), block(p, xm(-d), y, Y_COLS))
            send(
                ("YxF", s, d), block(p, xm(-d), y, Y_COLS, half, RB // 2), at_x(d)
            )

    def stage_c(s):
        p = plane_at(s)
        for d in (1, -1):
            half = 0 if d == 1 else RB // 2
            arrive(("XyF", s, d), block(p, x, ym(2), x_cols(s), half, RB // 2))
            arrive(("YxF", s, d), block(p, xm(2), y, Y_COLS, half, RB // 2))
        for d in (1, -1):
            send(("Xx", s, d), y_group(p, x, x_cols(s)), at_x(d))
            send(("Yy", s, d), x_group(p, y, Y_COLS), at_y(d))

    def stage_d(s):
        p = plane_at(s)
        for d in (1, -1):
            half = 0 if d == 1 else 1
            arrive(("Xx", s, d), y_group(p, xm(-d), x_cols(s)))
            send(
                ("XxF", s, d),
                y_group(p, xm(-d), x_cols(s), half * 2 * RB, 2 * RB),
                at_x(d),
            )
            arrive(("Yy", s, d), x_group(p, ym(-d), Y_COLS))
            send(
                ("YyF", s, d), x_group(p, ym(-d), Y_COLS, half * 2, 2), at_y(d)
            )

    def stage_e(s):
        p = plane_at(s)
        for d in (1, -1):
            half = 0 if d == 1 else 1
            arrive(
                ("XxF", s, d), y_group(p, xm(2), x_cols(s), half * 2 * RB, 2 * RB)
            )
            arrive(("YyF", s, d), x_group(p, ym(2), Y_COLS, half * 2, 2))

    def w_piece(h, g, d):
        return y_group(zm(-d * h), xm(W_OFF[g]), W_COLS)

    def w_final(g, d):
        return (g < 2) == (d == 1)

    def w_send(h, g, d):
        if h > 4 or (h == 4 and not w_final(g, d)):
            return
        send(("W", h, g, d), w_piece(h - 1, g, d), at_z(d))

    def w_arrive(h, g, d):
        if h > 4 or (h == 4 and not w_final(g, d)):
            return
        arrive(("W", h, g, d), w_piece(h, g, d))

    def zb_cols(h, d):
        return ZB_COLS if h < 4 else (Y_COLS if d == 1 else X_COLS)

    def z_send(h, d):
        send(
            ("Z", h, d), block(zm(-d * (h - 1)), x, y, zb_cols(h, d)), at_z(d)
        )

    def z_arrive(h, d):
        arrive(("Z", h, d), block(zm(-d * h), x, y, zb_cols(h, d)))

    def plane_ref(s, cc):
        return buf.at[pl.ds((plane_at(s) * 2 + cc) * NX, NX)]

    def comm(t):
        both = (1, -1)
        if t == 0:
            stage_a(0)
            for d in both:
                z_send(1, d)
            for d in (1, 2, 3):
                send(("Sy", d), sbuf.at[z, core, x * NY + y], at_y(d))
            return
        if t == 1:
            for d in both:
                z_arrive(1, d)
                z_send(2, d)
            stage_b(0)
            stage_a(1)
            for d in (1, 2, 3):
                arrive(("Sy", d), sbuf.at[z, core, x * NY + ym(-d)])
            for d in (1, 2, 3):
                send(("Sx", d), sbuf.at[z, core, pl.ds(x * NY, NY)], at_x(d))
            return
        if 0 <= t - 4 < SLOTS:
            stage_e(t - 4)
        if t == 2:
            for d in both:
                z_arrive(2, d)
                z_send(3, d)
        if t == 3:
            for d in both:
                z_arrive(3, d)
                z_send(4, d)
        if t == 4:
            for d in both:
                z_arrive(4, d)
            for d in both:
                w_send(1, 3, d)
        if 4 <= t <= 10:
            for n in (2 * (t - 4), 2 * (t - 4) + 1):
                h, g = n // 4 + 1, n % 4
                if t < 10:
                    for d in both:
                        w_arrive(h, g, d)
                        w_send(h + 1, g, d)
            if t == 10:
                for g in range(4):
                    for d in both:
                        w_arrive(4, g, d)
        if 0 <= t - 4 < SLOTS:
            send(("D", t - 4), plane_ref(t - 4, core), sibling)
        if 0 <= t - 3 < SLOTS:
            stage_d(t - 3)
        if t == 3:
            for g in (1, 2):
                for d in both:
                    w_send(1, g, d)
        if 0 <= t - 2 < SLOTS:
            stage_c(t - 2)
        if t == 2:
            for d in both:
                w_send(1, 0, d)
        if 0 <= t - 1 < SLOTS:
            stage_b(t - 1)
        if t < SLOTS:
            stage_a(t)
        if t == 2:
            for d in (1, 2, 3):
                arrive(("Sx", d), sbuf.at[z, core, pl.ds(xm(-d) * NY, NY)])
            for d in range(1, NZ):
                send(("Sz", d), sbuf.at[z, core], at_z(d))
        if t == 3:
            for d in range(1, NZ):
                arrive(("Sz", d), sbuf.at[zm(-d), core])
            send(("Sd",), sbuf.at[:, core], sibling)
        if t == 4:
            arrive(("Sd",), sbuf.at[:, 1 - core])
        if 0 <= t - 5 < SLOTS:
            arrive(("D", t - 5), plane_ref(t - 5, 1 - core))

    def codes_of(plane, cc):
        return buf[pl.ds((plane * 2 + cc) * NX, NX)].reshape(NX * NY * RB, width)

    def scores(plane, cc, out):
        codes = codes_of(plane, cc)
        for first in range(0, q_ref.shape[0], ROWS):
            rows = pl.ds(first, ROWS)
            out[rows, :] = lax.dot_general(
                q_ref[rows, :],
                codes,
                (((1,), (1,)), ((), ())),
                preferred_element_type=jnp.float32,
            )

    def fold(values, op):
        out = values[:, 0:128]
        for j in range(1, values.shape[1] // 128):
            out = op(out, values[:, j * 128 : (j + 1) * 128])
        return out

    def consume(plane, cc, raw):
        codes = codes_of(plane, cc)
        count = codes.shape[0]
        by_y = sbuf[plane, cc]
        scales = jnp.concatenate(
            [jnp.sum(by_y[i * NY : (i + 1) * NY], axis=0) for i in range(NX)], axis=1
        )
        factor = scales * (temper * LOG2E)
        start = (plane * 2 + cc) * count
        for first in range(0, q_ref.shape[0], ROWS):
            rows = pl.ds(first, ROWS)
            s = raw[rows, :] * factor
            old = run_max[rows, :]
            new = jnp.maximum(
                old, jnp.max(fold(s, jnp.maximum), axis=1, keepdims=True)
            )
            run_max[rows, :] = new
            alpha = jnp.exp2(old - new)
            p = jnp.exp2(s - new[:, 0:1])
            hit = lax.broadcasted_iota(jnp.int32, s.shape, 1) == (
                pos[rows, 0:1] - start
            )
            run_sum[rows, :] = run_sum[rows, :] * alpha + fold(p, jnp.add)
            chosen[rows, :] += fold(jnp.where(hit, s, 0.0), jnp.add)
            weights = jnp.where(hit, 0.0, p * scales).astype(jnp.bfloat16)
            onehot = jnp.where(hit, scales, 0.0).astype(jnp.bfloat16)
            spread = jnp.concatenate([alpha] * (width // 128), axis=1)
            acc[rows, :] = acc[rows, :] * spread + jnp.dot(
                weights, codes, preferred_element_type=jnp.float32
            )
            picked[rows, :] += jnp.dot(
                onehot, codes, preferred_element_type=jnp.float32
            )

    def diagonal():
        shape = (128, 128)
        return lax.broadcasted_iota(jnp.int32, shape, 0) == lax.broadcasted_iota(
            jnp.int32, shape, 1
        )

    def prepare():
        j = p_ref[...]
        device = j // RB
        w = device // 4
        jz = lax.rem(device, 4) * 2 + w // 32
        flat = (
            (jz * 2 + lax.rem(w, 2)) * NX + lax.rem(w // 8, NX)
        ) * (NY * RB) + lax.rem(w // 2, NY) * RB + lax.rem(j, RB)
        flat = flat.astype(jnp.float32)
        for i in range(flat.shape[0]):
            column = jnp.sum(
                jnp.where(diagonal(), flat[i : i + 1, :], 0.0), axis=1, keepdims=True
            )
            pos[pl.ds(i * 128, 128), :] = jnp.broadcast_to(
                column, (128, 128)
            ).astype(jnp.int32)
        run_max[...] = jnp.full_like(run_max, -1e30)
        run_sum[...] = jnp.zeros_like(run_sum)
        chosen[...] = jnp.zeros_like(chosen)
        acc[...] = jnp.zeros_like(acc)
        picked[...] = jnp.zeros_like(picked)

    comm(0)
    prepare()
    for t in range(1, 5):
        comm(t)
    scores(plane_at(0), core, s_a)

    last = SLOTS + 4

    def tick(t, carry):
        for k in range(5, last + 1):

            @pl.when(t == k)
            def _():
                comm(k)

        def plane_dyn(s):
            k = (s + 1) // 2
            return lax.rem(z + k * (1 - 2 * lax.rem(s, 2)) + NZ, NZ)

        here = plane_dyn(t - 5)
        after = plane_dyn(jnp.minimum(t - 4, SLOTS - 1))
        scores(here, 1 - core, s_b)
        consume(here, core, s_a)
        scores(after, core, s_a)
        consume(here, 1 - core, s_b)
        return carry

    lax.fori_loop(5, last + 1, tick, 0)
    draining.append(True)
    for t in range(last + 1):
        comm(t)
    assert len(index) == n_copies, len(index)

    total = jnp.sum(run_sum[...], axis=1, keepdims=True)
    lse = run_max[:, 0:1] + jnp.log2(total)
    score = jnp.sum(chosen[...], axis=1, keepdims=True)
    losses = (lse - score) * (1.0 / LOG2E)
    for i in range(loss_ref.shape[0]):
        loss_ref[pl.ds(i, 1), :] = jnp.sum(
            jnp.where(diagonal(), losses[i * 128 : (i + 1) * 128], 0.0),
            axis=0,
            keepdims=True,
        )
    extra = jnp.exp2(score - lse) - 1.0
    inverse = 1.0 / total
    grad_ref[...] = (temper * (acc[...] * inverse + extra * picked[...])).astype(
        grad_ref.dtype
    )


N_COPIES = 186


def shards(queries, documents, positives):
    count, width = queries.shape
    vmem = pl.BlockSpec(memory_space=pltpu.VMEM)
    f32 = jnp.float32
    losses, grad = pl.pallas_call(
        lambda *refs: kernel(N_COPIES, *refs),
        out_shape=(
            jax.ShapeDtypeStruct((count // 128, 128), f32),
            jax.ShapeDtypeStruct((count, width), queries.dtype),
        ),
        in_specs=[vmem] * 3,
        out_specs=(vmem, vmem),
        scratch_shapes=[
            pltpu.VMEM((NZ * 2 * NX, NY * RB, width), jnp.bfloat16),
            pltpu.VMEM((NZ, 2, NX * NY, 1, 128), f32),
            pltpu.VMEM((count, 128), jnp.int32),
            pltpu.VMEM((count, 128), f32),
            pltpu.VMEM((count, 128), f32),
            pltpu.VMEM((count, 128), f32),
            pltpu.VMEM((count, width), f32),
            pltpu.VMEM((count, width), f32),
            pltpu.VMEM((count, 512), f32),
            pltpu.VMEM((count, 512), f32),
            pltpu.SemaphoreType.DMA((N_COPIES,)),
            pltpu.SemaphoreType.DMA((N_COPIES,)),
        ],
        compiler_params=pltpu.CompilerParams(
            collective_id=0, has_side_effects=True, vmem_limit_bytes=56 * 2**20
        ),
        name="gather_softmax",
    )(queries, documents, positives.reshape(count // 128, 128))
    return losses.reshape(count), grad


def solution(mesh):
    placed = (P(("wide", "narrow"), None), P(("wide", "narrow"), None), P(("wide", "narrow")))
    return jax.shard_map(
        shards,
        mesh=mesh,
        in_specs=placed,
        out_specs=(P(("wide", "narrow")), P(("wide", "narrow"), None)),
        check_vma=False,
    )
```

time: 249 us -> 75.2 us (0.30)
  blocking collectives: 102 us -> 0 us
  matrix products: 86.3 us -> 0 us
  Pallas kernels: 0 us -> 71.1 us
  waiting for transfers between devices: 29 us -> 0 us
  between operations: 14.1 us -> 0.65 us
  other arithmetic: 8.24 us -> 0 us
  starting transfers between devices: 3.38 us -> 0 us
    dot_general x32 -> x0, matrix products: 86.3 us -> none  [the longest x16 54.5 us: gradient(): return total + jnp.dot(weights, piece, preferred_element_type=jnp.float32)]
    all_gather x1 -> x0, blocking collectives: 85.3 us -> none  [shards(): lax.all_gather(group_scales.astype(jnp.bfloat16), 'wide', axis=0, tiled=T...]
    pallas_call x0 -> x1, Pallas kernels: none -> 71.1 us  [shards(): pl.pallas_call(lambda *refs: kernel(N_COPIES, *refs), out_shape=(jax.Shap...]
    all_gather x1 -> x0, waiting for transfers between devices: 22.5 us -> none  [shards(): lax.all_gather(group_codes, 'wide', axis=0, tiled=True)]
    all_to_all x1 -> x0, blocking collectives: 17 us -> none  [copy_for_each(): lax.all_to_all(jnp.broadcast_to(shard[None], (peers, *shard.shape)), axis...]
    all_to_all x1 -> x0, waiting for transfers between devices: 6.46 us -> none  [copy_for_each(): lax.all_to_all(jnp.broadcast_to(shard[None], (peers, *shard.shape)), axis...]
    reduce_sum x16 -> x0, other arithmetic: 4.25 us -> none  [totals(): chosen = chosen + jnp.sum(jnp.where(found, scores, 0.0), axis=1)]
    all_to_all x1 -> x0, starting transfers between devices: 3.34 us -> none  [copy_for_each(): lax.all_to_all(jnp.broadcast_to(shard[None], (peers, *shard.shape)), axis...]
  transfers between devices with their start and end apart: 2 -> 0, of which waited for: 2 -> 0; matrix products, arithmetic and copies ran while one was open for 0% -> 0% of each run, Pallas kernels for 0% -> 0%
where the time goes in v1:
time: 75.2 us; the launch traced here: 75 us
  Pallas kernels  71.1 us (95%)
  local copies, waits for them, and re-layouts  3.29 us (4%)
    pallas_call x1, Pallas kernels, shards(): pl.pallas_call(lambda *refs: kernel(N_COPIES, *refs), out_shape=(jax.Shap...  71.1 us
    unnamed x4, local copies, waits for them, and re-layouts  3.29 us

profile of v1, /device:TPU:1, one launch (start us, length us, event | category | flops | bytes accessed | tf_op | source)
XLA Modules:
  0.0 75.0 jit_solution(18317355642343204285)
XLA Ops:
  0.6 71.1 %gather_softmax.1 = (f32[4,128]{1,0:T(4,128)}, bf16[512,768]{1,0:T(8,128)(2,1)}) custom-call(bf16[512,768]{1,0:T(8,128)(2,1)} %refs_0_.1, bf16[32,768]{1,0:T(8,128)(2,1)} %refs_1_.1, s32[4,128]{1,0:T(4,128)} %bitcast.2), custom_call_target="tpu_custom_call" | custom-call | tf_op jit(solution)/shard_map/gather_softmax/pallas_call | solution.py:441
  71.7 0.0 copy-start
  71.7 0.6 copy-done
  72.4 0.6 copy.7
  72.9 2.1 %copy.8 = bf16[512,768]{1,0:T(8,128)(2,1)} copy(bf16[512,768]{1,0:T(8,128)(2,1)} %get-tuple-element.9) | data formatting | bytes 1572864
Async XLA Ops:
  71.7 0.7 copy-start

commit v2 on v1

v2 whole, which is shorter than its diff:
```python
import jax
import jax.numpy as jnp
import numpy as np
from jax import lax
from jax.experimental import pallas as pl
from jax.experimental.pallas import tpu as pltpu
from jax.sharding import PartitionSpec as P

LOG2E = 1.4426950408889634
MESH = pl.DeviceIdType.MESH
NX, NY, NZ = 4, 4, 8
RB = 32
SLOTS = 8
Y_COLS = (0, 256)
X_COLS = (256, 256)
Y0_COLS = (0, 384)
X0_COLS = (384, 384)
W_COLS = (512, 256)
ZB_COLS = (0, 512)
W_OFF = (0, 1, 3, 2)
ROWS = 256
PLAN = (
    (("A", 0), ("Z", 1),),
    (("Z", 2), ("A", 1), ("A", 2), ("C", 0), ("W", 1, 0), ("B", 1), ("Z", 3), ("A", 3), ("B", 2), ("A", 4), ("W", 2, 0), ("D", 0), ("Z", 4), ("W", 1, 1), ("W", 1, 2), ("C", 1), ("A", 5), ("A", 6), ("B", 3), ("C", 2), ("B", 4), ("W", 3, 0), ("E", 0), ("W", 1, 3), ("A", 7),),
    (("D", 1), ("W", 2, 1),),
    (("W", 2, 2), ("C", 3), ("B", 5), ("B", 6), ("D", 2), ("C", 4), ("B", 7), ("W", 4, 0), ("E", 1), ("W", 2, 3),),
    (("D", 3), ("W", 3, 1), ("C", 5),),
    (("E", 2), ("W", 3, 2),),
    (("E", 3), ("D", 4), ("C", 6), ("W", 5, 0),),
    (("W", 3, 3), ("D", 5), ("C", 7),),
    (("E", 4), ("W", 4, 1),),
    (("D", 6), ("E", 5), ("W", 4, 2),),
    (("W", 4, 3), ("D", 7),),
    (("E", 6), ("W", 5, 1),),
    (("E", 7), ("W", 5, 2),),
    (("W", 5, 3),),
    (),
    (),
    (),
    (),
)


def kernel(
    q_ref,
    d_ref,
    p_ref,
    loss_ref,
    grad_ref,
    buf,
    sbuf,
    pos,
    run_max,
    run_sum,
    chosen,
    acc,
    picked,
    s_a,
    s_b,
    send_sem,
    recv_sem,
):
    wide = lax.axis_index("wide")
    narrow = lax.axis_index("narrow")
    core = lax.rem(wide, 2)
    y = lax.rem(wide // 2, NY)
    x = lax.rem(wide // 8, NX)
    z = narrow * 2 + wide // 32
    width = q_ref.shape[1]
    temper = width**-0.5

    def xm(d):
        return lax.rem(x + d + NX, NX)

    def ym(d):
        return lax.rem(y + d + NY, NY)

    def zm(d):
        return lax.rem(z + d + NZ, NZ)

    def dev(xx, yy, zz, cc):
        return ((lax.rem(zz, 2) * NX + xx) * NY + yy) * 2 + cc, zz // 2

    at_x = lambda d: dev(xm(d), y, z, core)
    at_y = lambda d: dev(x, ym(d), z, core)
    at_z = lambda d: dev(x, y, zm(d), core)
    sibling = dev(x, y, z, 1 - core)

    docs = d_ref[...].astype(jnp.float32)
    scale = jnp.max(jnp.abs(docs), axis=1, keepdims=True) + 1e-06
    mine = (z * 2 + core) * NX + x
    my_rows = pl.ds(pl.multiple_of(y * RB, RB), RB)
    buf[mine, my_rows, :] = (docs / scale).astype(jnp.bfloat16)
    lane = lax.broadcasted_iota(jnp.int32, (RB, 128), 1)
    row = lax.broadcasted_iota(jnp.int32, (RB, 128), 0)
    sbuf[z, core, x * NY + y] = jnp.sum(
        jnp.where(lane == row + y * RB, scale, 0.0), axis=0, keepdims=True
    )

    barrier = pltpu.get_barrier_semaphore()
    peers = (
        [sibling]
        + [at_x(d) for d in (1, 2, 3)]
        + [at_y(d) for d in (1, 2, 3)]
        + [at_z(d) for d in range(1, NZ)]
    )
    for peer in peers:
        pl.semaphore_signal(barrier, inc=1, device_id=peer, device_id_type=MESH)
    pl.semaphore_wait(barrier, len(peers))

    recv_index = {}
    send_index = {}
    totals = {}
    waited = set()

    def send(group, lane, ref, peer):
        pltpu.make_async_remote_copy(
            src_ref=ref,
            dst_ref=ref,
            send_sem=send_sem.at[send_index.setdefault(lane, len(send_index))],
            recv_sem=recv_sem.at[recv_index.setdefault(group, len(recv_index))],
            device_id=peer,
            device_id_type=MESH,
        ).start()
        totals[lane] = totals.get(lane, 0) + int(np.prod(ref.shape)) * ref.dtype.itemsize

    def dummy(tiles):
        for rows, cols in ((128, 768), (128, 256), (64, 256), (16, 256)):
            unit = rows * cols // 4096
            if tiles % unit == 0 and tiles // unit <= buf.shape[0]:
                return buf.at[pl.ds(0, tiles // unit), pl.ds(0, rows), pl.ds(0, cols)]
        raise ValueError(tiles)

    def semaphore_copy(ref, send_at, recv_at):
        return pltpu.make_async_remote_copy(
            src_ref=ref,
            dst_ref=ref,
            send_sem=send_sem.at[send_at],
            recv_sem=recv_sem.at[recv_at],
            device_id=sibling,
            device_id_type=MESH,
        )

    def scale_ref(rows):
        if rows % 16:
            return sbuf.at[0, 0, pl.ds(0, rows)]
        return sbuf.at[pl.ds(0, rows // 16), 0]

    def arrived(group):
        k = group[0]
        if k == "sc":
            return scale_ref((0, 3, 12, 112, 128)[group[1]])
        s = group[1]
        if k == "A":
            size = 144 if s == 0 else 64
        elif k == "B":
            size = 32
        elif k == "C":
            size = 384 if s == 0 else 256
        elif k == "D":
            size = 192 if s == 0 else 128
        elif k == "Z":
            size = 64 if s < 4 else 32
        elif k == "W":
            size = 128 if s < 4 else 64
        else:
            size = 768
        return dummy(size // 8)

    def need(group):
        if group not in waited:
            waited.add(group)
            semaphore_copy(
                arrived(group), 0, recv_index.setdefault(group, len(recv_index))
            ).wait_recv()

    def cell(plane, xx):
        return (plane * 2 + core) * NX + xx

    def block(plane, xx, yy, cols, first=0, rows=RB):
        start = pl.multiple_of(yy * RB + first, 16)
        return buf.at[cell(plane, xx), pl.ds(start, rows), pl.ds(*cols)]

    def y_group(plane, xx, cols, first=0, rows=NY * RB):
        return buf.at[cell(plane, xx), pl.ds(first, rows), pl.ds(*cols)]

    def x_group(plane, yy, cols, first=0, many=NX):
        start = pl.multiple_of(yy * RB, RB)
        return buf.at[
            pl.ds(cell(plane, 0) + first, many), pl.ds(start, RB), pl.ds(*cols)
        ]

    def plane_at(s):
        k = (s + 1) // 2
        return zm(-k if s % 2 else k)

    def x_cols(s):
        return X0_COLS if s == 0 else X_COLS

    def y_cols(s):
        return Y0_COLS if s == 0 else Y_COLS

    def lane_of(kind, s):
        return (kind, min(s, 1))

    both = (1, -1)

    def stage_a(s):
        if s:
            need(("Z", (s + 1) // 2))
        p = plane_at(s)
        for d in both if s else (1, -1, 2):
            send(("A", s), lane_of("A", s), block(p, x, y, x_cols(s)), at_y(d))
            send(("A", s), lane_of("A", s), block(p, x, y, y_cols(s)), at_x(d))

    def stage_b(s):
        need(("A", s))
        p = plane_at(s)
        half = RB // 2
        for d in both:
            first = 0 if d == 1 else half
            send(
                ("B", s),
                lane_of("B", s),
                block(p, x, ym(-d), x_cols(s), first, half),
                at_y(d),
            )
            send(
                ("B", s),
                lane_of("B", s),
                block(p, xm(-d), y, y_cols(s), first, half),
                at_x(d),
            )

    def stage_c(s):
        need(("B", s) if s else ("A", s))
        p = plane_at(s)
        for d in both:
            send(("C", s), lane_of("C", s), y_group(p, x, x_cols(s)), at_x(d))
            send(("C", s), lane_of("C", s), x_group(p, y, y_cols(s)), at_y(d))

    def over(s, ref):
        send(("S", s), ("S",), ref, sibling)

    def stage_d(s):
        need(("C", s))
        p = plane_at(s)
        for d in both:
            first = 0 if d == 1 else 2
            send(
                ("D", s),
                lane_of("D", s),
                y_group(p, xm(-d), x_cols(s), first * RB, 2 * RB),
                at_x(d),
            )
            send(
                ("D", s),
                lane_of("D", s),
                x_group(p, ym(-d), y_cols(s), first, 2),
                at_y(d),
            )
        for d in (0, 1, -1):
            over(s, y_group(p, xm(d), x_cols(s)))
            over(s, x_group(p, ym(d), y_cols(s)))

    def stage_e(s):
        need(("D", s))
        p = plane_at(s)
        over(s, y_group(p, xm(2), x_cols(s)))
        over(s, x_group(p, ym(2), y_cols(s)))

    def stage_w(h, g):
        if h == 1:
            need((("A", 0), ("C", 0), ("C", 0), ("D", 0))[g])
        else:
            need(("W", h - 1, g))
        for d in both:
            final = (g < 2) == (d == 1)
            piece = y_group(zm(-d * (h - 1)), xm(W_OFF[g]), W_COLS)
            if h < 4 or (h == 4 and final):
                send(("W", h, g), ("W",), piece, at_z(d))
            if h > 1 and (h < 5 or final):
                over(2 * (h - 1) - (1 if d == 1 or h == 5 else 0), piece)

    def stage_z(h):
        if h > 1:
            need(("Z", h - 1))
        for d in both:
            cols = ZB_COLS if h < 4 else (Y_COLS if d == 1 else X_COLS)
            send(("Z", h), ("Z",), block(zm(-d * (h - 1)), x, y, cols), at_z(d))
        if h > 1:
            need(("sc", h - 1))
        if h == 1:
            for d in (1, 2, 3):
                send(("sc", 1), ("sc", 1), sbuf.at[z, core, x * NY + y], at_y(d))
        elif h == 2:
            for d in (1, 2, 3):
                send(("sc", 2), ("sc", 2), sbuf.at[z, core, pl.ds(x * NY, NY)], at_x(d))
        elif h == 3:
            for d in range(1, NZ):
                send(("sc", 3), ("sc", 3), sbuf.at[z, core], at_z(d))
        else:
            send(("sc", 4), ("sc", 4), sbuf.at[:, core], sibling)

    stages = {
        "A": stage_a,
        "B": stage_b,
        "C": stage_c,
        "D": stage_d,
        "E": stage_e,
        "W": stage_w,
        "Z": stage_z,
    }

    def comm(point):
        for step in PLAN[point]:
            stages[step[0]](*step[1:])

    def drain():
        for lane, i in send_index.items():
            size = totals[lane]
            ref = scale_ref(size // 512) if lane[0] == "sc" else dummy(size // 8192)
            semaphore_copy(ref, i, 0).wait_send()

    def codes_of(plane, cc):
        return buf[pl.ds((plane * 2 + cc) * NX, NX)].reshape(NX * NY * RB, width)

    def scores(plane, cc, out):
        codes = codes_of(plane, cc)
        for first in range(0, q_ref.shape[0], ROWS):
            rows = pl.ds(first, ROWS)
            out[rows, :] = lax.dot_general(
                q_ref[rows, :],
                codes,
                (((1,), (1,)), ((), ())),
                preferred_element_type=jnp.float32,
            )

    def fold(values, op):
        out = values[:, 0:128]
        for j in range(1, values.shape[1] // 128):
            out = op(out, values[:, j * 128 : (j + 1) * 128])
        return out

    def consume(plane, cc, raw):
        codes = codes_of(plane, cc)
        count = codes.shape[0]
        by_y = sbuf[plane, cc]
        scales = jnp.concatenate(
            [jnp.sum(by_y[i * NY : (i + 1) * NY], axis=0) for i in range(NX)], axis=1
        )
        factor = scales * (temper * LOG2E)
        start = (plane * 2 + cc) * count
        for first in range(0, q_ref.shape[0], ROWS):
            rows = pl.ds(first, ROWS)
            s = raw[rows, :] * factor
            old = run_max[rows, :]
            new = jnp.maximum(
                old, jnp.max(fold(s, jnp.maximum), axis=1, keepdims=True)
            )
            run_max[rows, :] = new
            alpha = jnp.exp2(old - new)
            p = jnp.exp2(s - new[:, 0:1])
            hit = lax.broadcasted_iota(jnp.int32, s.shape, 1) == (
                pos[rows, 0:1] - start
            )
            run_sum[rows, :] = run_sum[rows, :] * alpha + fold(p, jnp.add)
            chosen[rows, :] += fold(jnp.where(hit, s, 0.0), jnp.add)
            weights = jnp.where(hit, 0.0, p * scales).astype(jnp.bfloat16)
            onehot = jnp.where(hit, scales, 0.0).astype(jnp.bfloat16)
            spread = jnp.concatenate([alpha] * (width // 128), axis=1)
            acc[rows, :] = acc[rows, :] * spread + jnp.dot(
                weights, codes, preferred_element_type=jnp.float32
            )
            picked[rows, :] += jnp.dot(
                onehot, codes, preferred_element_type=jnp.float32
            )

    def diagonal():
        shape = (128, 128)
        return lax.broadcasted_iota(jnp.int32, shape, 0) == lax.broadcasted_iota(
            jnp.int32, shape, 1
        )

    def prepare():
        j = p_ref[...]
        device = j // RB
        w = device // 4
        jz = lax.rem(device, 4) * 2 + w // 32
        flat = (
            (jz * 2 + lax.rem(w, 2)) * NX + lax.rem(w // 8, NX)
        ) * (NY * RB) + lax.rem(w // 2, NY) * RB + lax.rem(j, RB)
        flat = flat.astype(jnp.float32)
        for i in range(flat.shape[0]):
            column = jnp.sum(
                jnp.where(diagonal(), flat[i : i + 1, :], 0.0), axis=1, keepdims=True
            )
            pos[pl.ds(i * 128, 128), :] = jnp.broadcast_to(
                column, (128, 128)
            ).astype(jnp.int32)
        run_max[...] = jnp.full_like(run_max, -1e30)
        run_sum[...] = jnp.zeros_like(run_sum)
        chosen[...] = jnp.zeros_like(chosen)
        acc[...] = jnp.zeros_like(acc)
        picked[...] = jnp.zeros_like(picked)

    comm(0)
    prepare()
    comm(1)
    scores(plane_at(0), core, s_a)

    def tick(t, carry):
        k = (t + 1) // 2
        here = lax.rem(z + k * (1 - 2 * lax.rem(t, 2)) + NZ, NZ)
        t1 = jnp.minimum(t + 1, SLOTS - 1)
        k = (t1 + 1) // 2
        after = lax.rem(z + k * (1 - 2 * lax.rem(t1, 2)) + NZ, NZ)
        for i in range(SLOTS):

            @pl.when(t == i)
            def _():
                comm(2 * i + 2)
                if i == 0:
                    need(("sc", 4))
                need(("S", i))

        scores(here, 1 - core, s_b)
        consume(here, core, s_a)
        for i in range(SLOTS - 1):
            if PLAN[2 * i + 3]:

                @pl.when(t == i)
                def _():
                    comm(2 * i + 3)

        scores(after, core, s_a)
        consume(here, 1 - core, s_b)
        return carry

    lax.fori_loop(0, SLOTS, tick, 0)
    drain()
    assert (len(send_index), len(recv_index)) == (N_SEND, N_RECV)

    total = jnp.sum(run_sum[...], axis=1, keepdims=True)
    lse = run_max[:, 0:1] + jnp.log2(total)
    score = jnp.sum(chosen[...], axis=1, keepdims=True)
    losses = (lse - score) * (1.0 / LOG2E)
    for i in range(loss_ref.shape[0]):
        loss_ref[pl.ds(i, 1), :] = jnp.sum(
            jnp.where(diagonal(), losses[i * 128 : (i + 1) * 128], 0.0),
            axis=0,
            keepdims=True,
        )
    extra = jnp.exp2(score - lse) - 1.0
    inverse = 1.0 / total
    grad_ref[...] = (temper * (acc[...] * inverse + extra * picked[...])).astype(
        grad_ref.dtype
    )


N_SEND = 14
N_RECV = 63


def shards(queries, documents, positives):
    count, width = queries.shape
    vmem = pl.BlockSpec(memory_space=pltpu.VMEM)
    f32 = jnp.float32
    losses, grad = pl.pallas_call(
        kernel,
        out_shape=(
            pltpu.VMEM((count // 128, 128), f32),
            pltpu.VMEM((count, width), queries.dtype),
        ),
        in_specs=[vmem] * 3,
        out_specs=(vmem, vmem),
        scratch_shapes=[
            pltpu.VMEM((NZ * 2 * NX, NY * RB, width), jnp.bfloat16),
            pltpu.VMEM((NZ, 2, NX * NY, 1, 128), f32),
            pltpu.VMEM((count, 128), jnp.int32),
            pltpu.VMEM((count, 128), f32),
            pltpu.VMEM((count, 128), f32),
            pltpu.VMEM((count, 128), f32),
            pltpu.VMEM((count, width), f32),
            pltpu.VMEM((count, width), f32),
            pltpu.VMEM((count, 512), f32),
            pltpu.VMEM((count, 512), f32),
            pltpu.SemaphoreType.DMA((N_SEND,)),
            pltpu.SemaphoreType.DMA((N_RECV,)),
        ],
        compiler_params=pltpu.CompilerParams(
            collective_id=0, has_side_effects=True, vmem_limit_bytes=56 * 2**20
        ),
        name="gather_softmax",
    )(queries, documents, positives.reshape(count // 128, 128))
    return losses.reshape(count), grad


def solution(mesh):
    placed = (P(("wide", "narrow"), None), P(("wide", "narrow"), None), P(("wide", "narrow")))
    return jax.shard_map(
        shards,
        mesh=mesh,
        in_specs=placed,
        out_specs=(P(("wide", "narrow")), P(("wide", "narrow"), None)),
        check_vma=False,
    )
```

time: 75.2 us -> 62.7 us (0.83)
  Pallas kernels: 71.1 us -> 60.5 us
  local copies, waits for them, and re-layouts: 3.29 us -> 1.46 us
    pallas_call x1, Pallas kernels: 71.1 us -> 60.5 us  [shards(): pl.pallas_call(kernel, out_shape=(pltpu.VMEM((count // 128, 128), f32), p...]
    unnamed x4 -> x2, local copies, waits for them, and re-layouts: 3.29 us -> 1.46 us
where the time goes in v2:
time: 62.7 us; the launch traced here: 62.6 us
  Pallas kernels  60.5 us (96%)
  local copies, waits for them, and re-layouts  1.46 us (2%)
  between operations  0.64 us (1%)
    pallas_call x1, Pallas kernels, shards(): pl.pallas_call(kernel, out_shape=(pltpu.VMEM((count // 128, 128), f32), p...  60.5 us
    unnamed x2, local copies, waits for them, and re-layouts  1.46 us

profile of v2, /device:TPU:1, one launch (start us, length us, event | category | flops | bytes accessed | tf_op | source)
XLA Modules:
  0.0 62.6 jit_solution(10732409071365072682)
XLA Ops:
  0.6 60.5 %gather_softmax.1 = (f32[4,128]{1,0:T(4,128)S(1)}, bf16[512,768]{1,0:T(8,128)(2,1)S(1)}) custom-call(bf16[512,768]{1,0:T(8,128)(2,1)} %q_ref.1, bf16[32,768]{1,0:T(8,128)(2,1)} %d_ref.1, s32[4,128]{1,0:T(4,128)} %bitcast.3), custom_call_target="tpu_custom_call" | custom-call | tf_op jit(solution)/shard_map/gather_softmax/pallas_call | solution.py:469
  61.2 0.6 copy.7
  61.8 0.9 %copy.8 = bf16[512,768]{1,0:T(8,128)(2,1)} copy(bf16[512,768]{1,0:T(8,128)(2,1)S(1)} %get-tuple-element.7) | data formatting | bytes 1572864

commit v3 on v0

v3 whole, which is shorter than its diff:
```python
import jax
import jax.numpy as jnp
import numpy as np
from jax import lax
from jax.experimental import pallas as pl
from jax.experimental.pallas import tpu as pltpu
from jax.sharding import PartitionSpec as P

LOG2E = 1.4426950408889634
MESH = pl.DeviceIdType.MESH
NX, NY, NZ = 4, 4, 8
RB = 32
CHIPS = NX * NY * NZ
PER = 8
CHUNKS = CHIPS // PER
ROWS = 256
UNITS = RB * 768 * 2 // 512 + 1
LANE_BLOCKS = 10

OFFSETS = (
    (0, 0, 0), (1, 0, 0), (3, 0, 0), (0, 1, 0), (0, 3, 0), (0, 0, 1), (0, 0, 7), (2, 0, 0),
    (0, 2, 0), (0, 0, 6), (1, 1, 0), (3, 1, 0), (0, 1, 1), (1, 3, 0), (1, 0, 7), (1, 0, 1),
    (3, 3, 0), (0, 1, 7), (0, 3, 1), (0, 0, 2), (3, 0, 7), (3, 0, 1), (0, 3, 7), (0, 0, 4),
    (1, 2, 0), (3, 2, 0), (2, 1, 0), (2, 0, 1), (2, 0, 7), (2, 3, 0), (0, 2, 1), (0, 2, 7),
    (0, 1, 6), (1, 0, 6), (3, 0, 6), (0, 3, 6), (0, 1, 2), (1, 1, 1), (0, 0, 5), (3, 1, 1),
    (1, 3, 1), (1, 1, 7), (0, 3, 2), (1, 3, 7), (1, 0, 2), (3, 0, 2), (0, 0, 3), (0, 1, 4),
    (1, 0, 4), (3, 3, 7), (3, 1, 7), (3, 3, 1), (2, 0, 2), (1, 2, 1), (2, 1, 1), (0, 1, 5),
    (3, 2, 1), (2, 3, 1), (0, 2, 2), (1, 2, 7), (2, 1, 7), (1, 0, 5), (3, 2, 7), (2, 3, 7),
    (0, 1, 3), (1, 1, 6), (3, 1, 6), (3, 0, 5), (3, 3, 6), (1, 3, 6), (1, 1, 2), (2, 0, 6),
    (0, 2, 6), (0, 3, 5), (3, 1, 2), (2, 2, 0), (0, 3, 3), (1, 3, 2), (0, 2, 4), (1, 0, 3),
    (3, 0, 3), (3, 3, 2), (2, 0, 4), (1, 1, 4), (2, 0, 3), (1, 2, 6), (3, 0, 4), (0, 3, 4),
    (2, 0, 5), (0, 2, 5), (0, 2, 3), (2, 1, 6), (3, 1, 5), (1, 3, 5), (1, 2, 2), (1, 1, 3),
    (2, 1, 2), (3, 3, 5), (3, 1, 3), (2, 3, 2), (3, 2, 2), (1, 1, 5), (3, 2, 6), (2, 3, 6),
    (2, 2, 1), (2, 2, 7), (1, 3, 3), (1, 2, 4), (3, 3, 3), (1, 3, 4), (2, 1, 3), (1, 2, 5),
    (2, 2, 6), (3, 2, 5), (2, 3, 3), (2, 1, 5), (2, 1, 4), (3, 1, 4), (2, 3, 5), (1, 2, 3),
    (3, 3, 4), (3, 2, 3), (2, 2, 2), (3, 2, 4), (2, 3, 4), (2, 2, 4), (2, 2, 3), (2, 2, 5),
)

GROUPS = (6, 1, 1, 1, 5, 6, 3, 4, 2, 2, 4, 4, 2, 4, 1, 2, 1, 2, 6, 6, 6, 6, 6, 2, 6, 4, 6, 6, 4, 5, 4, 6, 1, 2)

PLAN = (
    ((0, 0, 0, 1, 0), (0, 1, 0, 2, 0), (0, 2, 0, 3, 0), (0, 3, 0, 4, 0), (0, 4, 0, 5, 0), (0, 5, 0, 6, 0), (0, 6, 0, 23, 1), (0, 7, 0, 7, 2), (0, 8, 0, 8, 3), (2, 0, 1),),
    ((1, 0), (0, 5, 6, 9, 4), (0, 0, 3, 10, 4), (0, 1, 3, 11, 4), (0, 2, 5, 12, 4), (0, 3, 1, 13, 4), (2, 1, 7), (0, 5, 1, 14, 5), (0, 0, 5, 15, 5), (0, 1, 4, 16, 5), (0, 2, 6, 17, 5), (0, 3, 5, 18, 5), (0, 4, 5, 19, 5), (0, 5, 2, 20, 6), (0, 1, 5, 21, 6), (0, 3, 6, 22, 6), (1, 2), (0, 2, 7, 26, 7), (0, 4, 7, 27, 7), (0, 5, 7, 28, 7), (0, 3, 7, 29, 7), (2, 7, 8), (1, 3), (0, 0, 8, 24, 8), (0, 1, 8, 25, 8), (2, 8, 9), (0, 4, 8, 30, 9), (0, 5, 8, 31, 9), (1, 4), (0, 2, 9, 32, 10), (0, 0, 9, 33, 10), (0, 1, 9, 34, 10), (0, 3, 9, 35, 10), (2, 9, 14),),
    ((0, 4, 12, 36, 11), (0, 0, 12, 37, 11), (0, 5, 9, 38, 11), (0, 1, 12, 39, 11), (0, 4, 13, 40, 12), (0, 5, 10, 41, 12), (1, 5), (0, 3, 14, 43, 13), (0, 0, 19, 44, 13), (0, 1, 19, 45, 13), (0, 3, 19, 42, 14), (0, 4, 19, 46, 13), (2, 14, 16), (2, 16, 20), (0, 5, 16, 49, 15), (0, 1, 17, 50, 15), (1, 6), (0, 3, 21, 51, 16), (2, 20, 23), (1, 1), (0, 2, 23, 47, 17), (0, 0, 23, 48, 17), (2, 23, 24),),
    ((1, 8), (1, 7), (1, 9), (1, 10), (0, 4, 27, 52, 18), (0, 0, 30, 53, 18), (0, 2, 27, 54, 18), (0, 5, 32, 55, 18), (0, 1, 30, 56, 18), (0, 3, 27, 57, 18), (0, 4, 30, 58, 19), (0, 0, 31, 59, 19), (0, 2, 28, 60, 19), (0, 5, 33, 61, 19), (0, 1, 31, 62, 19), (0, 3, 28, 63, 19), (2, 24, 32), (2, 32, 36),),
    ((1, 11), (0, 4, 36, 64, 20), (0, 0, 32, 65, 20), (0, 2, 34, 66, 20), (0, 5, 34, 67, 20), (0, 1, 35, 68, 20), (0, 3, 33, 69, 20), (0, 4, 37, 70, 21), (0, 0, 33, 71, 21), (0, 2, 32, 72, 21), (0, 5, 35, 73, 21), (0, 1, 36, 74, 21), (0, 3, 29, 75, 21), (2, 36, 40), (1, 12), (2, 40, 42), (1, 14), (2, 42, 43),),
    ((1, 13), (1, 17), (1, 15), (1, 16), (0, 4, 42, 76, 22), (0, 0, 42, 77, 22), (0, 2, 47, 78, 22), (0, 5, 48, 79, 22), (0, 1, 46, 80, 22), (0, 3, 45, 81, 22), (0, 0, 48, 82, 23), (0, 2, 48, 83, 23), (2, 43, 48), (2, 48, 52),),
    ((1, 18), (1, 19), (0, 4, 52, 84, 24), (0, 5, 59, 85, 24), (0, 1, 23, 86, 24), (0, 3, 23, 87, 24), (0, 4, 58, 90, 25), (0, 0, 61, 88, 24), (0, 2, 55, 89, 24), (0, 5, 60, 91, 25), (0, 1, 55, 92, 25), (0, 3, 61, 93, 25), (2, 52, 56), (2, 56, 64),),
    ((1, 20), (0, 4, 53, 94, 26), (0, 0, 64, 95, 26), (0, 2, 52, 96, 26), (0, 5, 68, 97, 26), (0, 1, 64, 98, 26), (0, 3, 52, 99, 26), (0, 4, 56, 100, 27), (0, 0, 55, 101, 27), (0, 2, 66, 102, 27), (0, 5, 63, 103, 27), (0, 1, 56, 104, 27), (0, 3, 63, 105, 27), (2, 64, 70),),
    ((1, 21), (1, 22), (0, 4, 77, 106, 28), (0, 0, 78, 107, 28), (0, 1, 76, 108, 28), (0, 3, 48, 109, 28), (2, 70, 72), (2, 72, 80), (2, 80, 82),),
    ((1, 23), (1, 24), (0, 2, 84, 110, 29), (0, 5, 85, 111, 29), (0, 0, 85, 112, 29), (0, 1, 89, 113, 29), (0, 3, 84, 114, 29), (0, 2, 88, 115, 30), (0, 0, 83, 116, 30), (0, 1, 47, 117, 30), (0, 3, 88, 118, 30), (2, 82, 88), (2, 88, 90), (1, 25), (2, 90, 94),),
    ((1, 26), (0, 4, 94, 119, 31), (0, 5, 97, 120, 31), (0, 2, 98, 121, 31), (0, 0, 94, 122, 31), (0, 1, 78, 123, 31), (0, 3, 82, 124, 31), (2, 94, 96), (2, 96, 100),),
    ((1, 27), (1, 28), (0, 0, 107, 125, 32), (2, 100, 104), (2, 104, 110),),
    ((1, 29), (0, 2, 110, 126, 33), (0, 0, 111, 127, 33), (2, 110, 112), (2, 112, 115),),
    ((1, 30), (1, 31), (2, 115, 120), (2, 120, 125),),
    ((1, 32), (2, 125, 126),),
    ((1, 33), (2, 126, 128),),
    (),
    (),
)


N_SENT = sum(step[0] == 0 for point in PLAN for step in point)
N_LANES = -(-N_SENT // LANE_BLOCKS)


def offset_table():
    table = np.zeros((CHUNKS, PER * RB * 2), np.int32)
    for k in range(CHUNKS):
        for side in range(2):
            for b in range(PER):
                ox, oy, oz = OFFSETS[k * PER + b]
                first = (side * PER + b) * RB
                table[k, first : first + RB] = (
                    ox + oy * 4 + oz * 16 + side * 128 + np.arange(RB) * 256
                )
    return table


def kernel(
    q_hbm,
    d_ref,
    p_ref,
    table_ref,
    loss_ref,
    grad_ref,
    buf,
    sbuf,
    pos,
    ids,
    run_max,
    run_sum,
    chosen,
    acc,
    picked,
    s_a,
    s_b,
    q_ref,
    send_sem,
    recv_sem,
    load_sem,
):
    wide = lax.axis_index("wide")
    narrow = lax.axis_index("narrow")
    core = lax.rem(wide, 2)
    y = lax.rem(wide // 2, NY)
    x = lax.rem(wide // 8, NX)
    z = narrow * 2 + wide // 32
    width = q_ref.shape[1]
    temper = width**-0.5

    def dev(dx, dy, dz, cc):
        xx = lax.rem(x + dx + NX, NX)
        yy = lax.rem(y + dy + NY, NY)
        zz = lax.rem(z + dz + NZ, NZ)
        return ((lax.rem(zz, 2) * NX + xx) * NY + yy) * 2 + cc, zz // 2

    sibling = dev(0, 0, 0, 1 - core)
    peers = [
        dev(*d, core)
        for d in (
            (1, 0, 0),
            (-1, 0, 0),
            (0, 1, 0),
            (0, -1, 0),
            (0, 0, 1),
            (0, 0, -1),
            (0, 0, 4),
            (2, 0, 0),
            (0, 2, 0),
        )
    ]

    barrier = pltpu.get_barrier_semaphore()
    for peer in peers + [sibling]:
        pl.semaphore_signal(barrier, inc=1, device_id=peer, device_id_type=MESH)
    load = pltpu.make_async_copy(q_hbm, q_ref, load_sem)
    load.start()

    docs = d_ref[...].astype(jnp.float32)
    scale = jnp.max(jnp.abs(docs), axis=1, keepdims=True) + 1e-06
    buf[0, 0] = (docs / scale).astype(jnp.bfloat16)
    lane = lax.broadcasted_iota(jnp.int32, (RB, 128), 1)
    row = lax.broadcasted_iota(jnp.int32, (RB, 128), 0)
    sbuf[0] = jnp.sum(
        jnp.where((lane & (RB - 1)) == row, scale, 0.0), axis=0, keepdims=True
    )
    pl.semaphore_wait(barrier, len(peers) + 1)

    lanes = [0] * N_LANES
    count = [0]

    def remote(src, dst, send_at, recv_at, peer):
        return pltpu.make_async_remote_copy(
            src_ref=src,
            dst_ref=dst,
            send_sem=send_sem.at[send_at],
            recv_sem=recv_sem.at[recv_at],
            device_id=peer,
            device_id_type=MESH,
        )

    def whole(blocks):
        return sbuf.at[pl.ds(0, blocks * UNITS)]

    def send(direction, here, there, group):
        at = count[0] // LANE_BLOCKS
        count[0] += 1
        lanes[at] += 1
        peer = peers[direction]
        remote(buf.at[0, here], buf.at[0, there], at, group, peer).start()
        remote(sbuf.at[here], sbuf.at[there], at, group, peer).start()

    def arrive(group):
        ref = whole(GROUPS[group])
        remote(ref, ref, 0, group, sibling).wait_recv()

    def over(first, end):
        k, many = first // PER, end - first
        here, there = pl.ds(first, many), pl.ds(CHIPS + first, many)
        at, group = N_LANES + k, len(GROUPS) + k
        remote(buf.at[0, here], buf.at[1, here], at, group, sibling).start()
        remote(sbuf.at[here], sbuf.at[there], at, group, sibling).start()

    def comm(point):
        for step in PLAN[point]:
            (send, arrive, over)[step[0]](*step[1:])

    def chunk_here(k):
        ref = whole(PER)
        remote(ref, ref, 0, len(GROUPS) + k, sibling).wait_recv()

    def drain():
        for i, blocks in enumerate(lanes + [PER] * CHUNKS):
            ref = whole(blocks)
            remote(ref, ref, i, 0, sibling).wait_send()

    def codes_of(k):
        part = pl.ds(k * PER, PER)
        return jnp.concatenate(
            [buf[side, part].reshape(PER * RB, width) for side in range(2)], axis=0
        )

    def scores(k, out):
        codes = codes_of(k)
        for first in range(0, q_ref.shape[0], ROWS):
            rows = pl.ds(first, ROWS)
            out[rows, :] = lax.dot_general(
                q_ref[rows, :],
                codes,
                (((1,), (1,)), ((), ())),
                preferred_element_type=jnp.float32,
            )

    def fold(values, op):
        out = values[:, 0:128]
        for j in range(1, values.shape[1] // 128):
            out = op(out, values[:, j * 128 : (j + 1) * 128])
        return out

    def scales_of(k):
        quarter = lax.broadcasted_iota(jnp.int32, (1, 128), 1) // RB
        parts = []
        for side in range(2):
            for half in range(2):
                four = sbuf[pl.ds(side * CHIPS + k * PER + half * 4, 4)]
                part = four[0]
                for b in range(1, 4):
                    part = jnp.where(quarter == b, four[b], part)
                parts.append(part)
        return jnp.concatenate(parts, axis=1)

    def consume(k, raw):
        codes = codes_of(k)
        scales = scales_of(k)
        names = ids[pl.ds(k, 1), :]
        factor = scales * (temper * LOG2E)
        for first in range(0, q_ref.shape[0], ROWS):
            rows = pl.ds(first, ROWS)
            s = raw[rows, :] * factor
            old = run_max[rows, :]
            new = jnp.maximum(
                old, jnp.max(fold(s, jnp.maximum), axis=1, keepdims=True)
            )
            run_max[rows, :] = new
            alpha = jnp.exp2(old - new)
            p = jnp.exp2(s - new[:, 0:1])
            hit = names == pos[rows, 0:1]
            run_sum[rows, :] = run_sum[rows, :] * alpha + fold(p, jnp.add)
            chosen[rows, :] += fold(jnp.where(hit, s, 0.0), jnp.add)
            weights = jnp.where(hit, 0.0, p * scales).astype(jnp.bfloat16)
            onehot = jnp.where(hit, scales, 0.0).astype(jnp.bfloat16)
            spread = jnp.concatenate([alpha] * (width // 128), axis=1)
            acc[rows, :] = acc[rows, :] * spread + jnp.dot(
                weights, codes, preferred_element_type=jnp.float32
            )
            picked[rows, :] += jnp.dot(
                onehot, codes, preferred_element_type=jnp.float32
            )

    def diagonal():
        shape = (128, 128)
        return lax.broadcasted_iota(jnp.int32, shape, 0) == lax.broadcasted_iota(
            jnp.int32, shape, 1
        )

    def prepare():
        wanted = p_ref[...].astype(jnp.float32)
        for i in range(wanted.shape[0]):
            column = jnp.sum(
                jnp.where(diagonal(), wanted[i : i + 1, :], 0.0), axis=1, keepdims=True
            )
            pos[pl.ds(i * 128, 128), :] = jnp.broadcast_to(
                column, (128, 128)
            ).astype(jnp.int32)
        table = table_ref[...]
        sx = (x - (table & 3)) & 3
        sy = (y - ((table >> 2) & 3)) & 3
        sz = (z - ((table >> 4) & 7)) & 7
        sc = (core + ((table >> 7) & 1)) & 1
        device = ((((sz & 1) * NX + sx) * NY + sy) * 2 + sc) * 4 + (sz >> 1)
        ids[...] = device * RB + (table >> 8)
        run_max[...] = jnp.full_like(run_max, -1e30)
        run_sum[...] = jnp.zeros_like(run_sum)
        chosen[...] = jnp.zeros_like(chosen)
        acc[...] = jnp.zeros_like(acc)
        picked[...] = jnp.zeros_like(picked)

    comm(0)
    prepare()
    comm(1)
    load.wait()
    chunk_here(0)
    scores(0, s_a)

    def pair(t, carry):
        for i in range(CHUNKS // 2):

            @pl.when(t == i)
            def _():
                comm(2 * i + 2)
                chunk_here(2 * i + 1)

        scores(2 * t + 1, s_b)
        consume(2 * t, s_a)
        for i in range(CHUNKS // 2 - 1):

            @pl.when(t == i)
            def _():
                comm(2 * i + 3)
                chunk_here(2 * i + 2)

        scores(jnp.minimum(2 * t + 2, CHUNKS - 1), s_a)
        consume(2 * t + 1, s_b)
        return carry

    lax.fori_loop(0, CHUNKS // 2, pair, 0)
    drain()

    total = jnp.sum(run_sum[...], axis=1, keepdims=True)
    lse = run_max[:, 0:1] + jnp.log2(total)
    score = jnp.sum(chosen[...], axis=1, keepdims=True)
    losses = (lse - score) * (1.0 / LOG2E)
    for i in range(loss_ref.shape[0]):
        loss_ref[pl.ds(i, 1), :] = jnp.sum(
            jnp.where(diagonal(), losses[i * 128 : (i + 1) * 128], 0.0),
            axis=0,
            keepdims=True,
        )
    extra = jnp.exp2(score - lse) - 1.0
    inverse = 1.0 / total
    grad_ref[...] = (temper * (acc[...] * inverse + extra * picked[...])).astype(
        grad_ref.dtype
    )


def shards(queries, documents, positives):
    count, width = queries.shape
    vmem = pl.BlockSpec(memory_space=pltpu.VMEM)
    f32 = jnp.float32
    losses, grad = pl.pallas_call(
        kernel,
        out_shape=(
            pltpu.VMEM((count // 128, 128), f32),
            pltpu.VMEM((count, width), queries.dtype),
        ),
        in_specs=[pl.BlockSpec(memory_space=pltpu.HBM), vmem, vmem, vmem],
        out_specs=(vmem, vmem),
        scratch_shapes=[
            pltpu.VMEM((2, CHIPS, RB, width), jnp.bfloat16),
            pltpu.VMEM((LANE_BLOCKS * UNITS, 1, 128), f32),
            pltpu.VMEM((count, 128), jnp.int32),
            pltpu.VMEM((CHUNKS, PER * RB * 2), jnp.int32),
            pltpu.VMEM((count, 128), f32),
            pltpu.VMEM((count, 128), f32),
            pltpu.VMEM((count, 128), f32),
            pltpu.VMEM((count, width), f32),
            pltpu.VMEM((count, width), f32),
            pltpu.VMEM((count, PER * RB * 2), f32),
            pltpu.VMEM((count, PER * RB * 2), f32),
            pltpu.VMEM((count, width), queries.dtype),
            pltpu.SemaphoreType.DMA((N_LANES + CHUNKS,)),
            pltpu.SemaphoreType.DMA((len(GROUPS) + CHUNKS,)),
            pltpu.SemaphoreType.DMA,
        ],
        compiler_params=pltpu.CompilerParams(
            collective_id=0, has_side_effects=True, vmem_limit_bytes=56 * 2**20
        ),
        name="gather_softmax",
    )(
        queries,
        documents,
        positives.reshape(count // 128, 128),
        jnp.asarray(offset_table()),
    )
    return losses.reshape(count), grad


def solution(mesh):
    placed = (P(("wide", "narrow"), None), P(("wide", "narrow"), None), P(("wide", "narrow")))
    return jax.shard_map(
        shards,
        mesh=mesh,
        in_specs=placed,
        out_specs=(P(("wide", "narrow")), P(("wide", "narrow"), None)),
        check_vma=False,
    )
```

time: 249 us -> 53 us (0.21)
  blocking collectives: 102 us -> 0 us
  matrix products: 86.3 us -> 0 us
  Pallas kernels: 0 us -> 50.8 us
  waiting for transfers between devices: 29 us -> 0 us
  between operations: 14.1 us -> 0.64 us
  other arithmetic: 8.24 us -> 0 us
  starting transfers between devices: 3.38 us -> 0 us
    dot_general x32 -> x0, matrix products: 86.3 us -> none  [the longest x16 54.5 us: gradient(): return total + jnp.dot(weights, piece, preferred_element_type=jnp.float32)]
    all_gather x1 -> x0, blocking collectives: 85.3 us -> none  [shards(): lax.all_gather(group_scales.astype(jnp.bfloat16), 'wide', axis=0, tiled=T...]
    pallas_call x0 -> x1, Pallas kernels: none -> 50.8 us  [shards(): pl.pallas_call(kernel, out_shape=(pltpu.VMEM((count // 128, 128), f32), p...]
    all_gather x1 -> x0, waiting for transfers between devices: 22.5 us -> none  [shards(): lax.all_gather(group_codes, 'wide', axis=0, tiled=True)]
    all_to_all x1 -> x0, blocking collectives: 17 us -> none  [copy_for_each(): lax.all_to_all(jnp.broadcast_to(shard[None], (peers, *shard.shape)), axis...]
    all_to_all x1 -> x0, waiting for transfers between devices: 6.46 us -> none  [copy_for_each(): lax.all_to_all(jnp.broadcast_to(shard[None], (peers, *shard.shape)), axis...]
    reduce_sum x16 -> x0, other arithmetic: 4.25 us -> none  [totals(): chosen = chosen + jnp.sum(jnp.where(found, scores, 0.0), axis=1)]
    all_to_all x1 -> x0, starting transfers between devices: 3.34 us -> none  [copy_for_each(): lax.all_to_all(jnp.broadcast_to(shard[None], (peers, *shard.shape)), axis...]
  transfers between devices with their start and end apart: 2 -> 0, of which waited for: 2 -> 0; matrix products, arithmetic and copies ran while one was open for 0% -> 0% of each run, Pallas kernels for 0% -> 0%
where the time goes in v3:
time: 53 us; the launch traced here: 52.9 us
  Pallas kernels  50.8 us (96%)
  local copies, waits for them, and re-layouts  1.46 us (3%)
  between operations  0.64 us (1%)
    pallas_call x1, Pallas kernels, shards(): pl.pallas_call(kernel, out_shape=(pltpu.VMEM((count // 128, 128), f32), p...  50.8 us
    unnamed x2, local copies, waits for them, and re-layouts  1.46 us

profile of v3, /device:TPU:1, one launch (start us, length us, event | category | flops | bytes accessed | tf_op | source)
XLA Modules:
  0.0 52.9 jit_solution(9321850980950896444)
XLA Ops:
  0.6 50.8 %gather_softmax.1 = (f32[4,128]{1,0:T(4,128)S(1)}, bf16[512,768]{1,0:T(8,128)(2,1)S(1)}) custom-call(bf16[512,768]{1,0:T(8,128)(2,1)} %q_hbm.1, bf16[32,768]{1,0:T(8,128)(2,1)} %d_ref.1, s32[4,128]{1,0:T(4,128)} %bitcast.3, s32[16,512]{1,0:T(8,128)} %constant.2.clone.table_ref), custom_call_target="tpu_custom_call" | custom-call | tf_op jit(solution)/shard_map/gather_softmax/pallas_call | solution.py:341
  51.4 0.6 %copy.8 = f32[512]{0:T(512)} copy(f32[512]{0:T(512)S(1)} %bitcast.2) | data formatting | bytes 4096
  52.0 0.9 %copy.9 = bf16[512,768]{1,0:T(8,128)(2,1)} copy(bf16[512,768]{1,0:T(8,128)(2,1)S(1)} %get-tuple-element.7) | data formatting | bytes 1572864
